TPU v7x, 32 devices: a whole 2x2x4 slice. The times are simulated.
32 devices in a mesh: heads: 2 (over x), seq: 16 (over z, y, core).
Axes of the slice: x: 2, y: 2, z: 4, core: 2. Of those that a mesh axis runs over, the one named last changes fastest.
Arguments:
- q_nope: bfloat16 [1152, 64, 128], P('seq', 'heads'), may hold values from -6 to 6
- q_rope: bfloat16 [1152, 64, 64], P('seq', 'heads'), may hold values from -125 to 125
- latent: bfloat16 [1152, 512], P('seq'), may hold values from -6 to 6
- key_rope: bfloat16 [1152, 64], P('seq'), may hold values from -5 to 5
- absorb_key: bfloat16 [64, 128, 512], P('heads'), may hold values from -0.5 to 0.5
- absorb_value: bfloat16 [64, 512, 128], P('heads'), may hold values from -0.25 to 0.25
- w_out: bfloat16 [8192, 3584], P('heads', 'seq'), may hold values from -0.125 to 0.125
- residual: bfloat16 [1152, 3584], P(('seq', 'heads')), may hold values from -2 to 2
- norm_gain: float32 [3584], replicated, may hold values from 0.25 to 1.75
- span_table: int32 [32], replicated, may hold values from 0 to 31, each once
Outputs:
- new_residual: bfloat16 [1152, 3584], P(('seq', 'heads'))
- normed: bfloat16 [1152, 3584], P(('seq', 'heads'))
Inputs may be any that keep to these rules, and one draw needn't show every extreme that they name: `span_table`: A permutation of the span numbers.
All inputs are finite; a program needn't handle non-finite values.
Results may differ from a plain program's by a relative error of at most 0.014.
Values may be sent and summed in bfloat16 or wider, within the bound.
No kernel may reach another device: no remote copies, remote signals or barrier semaphores. Data moves between devices by JAX's collectives and lax.ppermute only.
A program may use at most 128 MiB of HBM per device.

v0:
```python
import jax
import jax.numpy as jnp
from jax import lax
from jax.sharding import PartitionSpec as P

score_scale = 192.0 ** (-0.5)


def place_rows(start, count, span_len, span_table):
    index = start + jnp.arange(count, dtype=jnp.int32)
    which = index // span_len
    picked = jnp.where(
        which[:, None] == jnp.arange(span_table.shape[0], dtype=jnp.int32)[None, :],
        span_table[None, :],
        0,
    )
    return jnp.sum(picked, axis=1) * span_len + index % span_len


def per_device(
    q_nope,
    q_rope,
    latent,
    key_rope,
    absorb_key,
    absorb_value,
    w_out,
    residual,
    norm_gain,
    span_table,
):
    tok_rows = q_nope.shape[0]
    span_len = tok_rows // 2
    seq_count = lax.axis_size("seq")
    my_start = lax.axis_index("seq") * tok_rows
    query_pos = place_rows(my_start, tok_rows, span_len, span_table)
    q_lat = jnp.einsum(
        "thd,hdl->htl", q_nope, absorb_key, preferred_element_type=jnp.float32
    ).astype(jnp.bfloat16)
    rotary = jnp.transpose(q_rope, (1, 0, 2))
    local_heads = q_lat.shape[0]

    def attend(carry, pieces, start):
        top, total, summed = carry
        lat_piece, rope_piece = pieces
        key_pos = place_rows(start, lat_piece.shape[0], span_len, span_table)
        score = jnp.einsum("htl,nl->htn", q_lat, lat_piece, preferred_element_type=jnp.float32)
        score = (
            score
            + jnp.einsum("htr,nr->htn", rotary, rope_piece, preferred_element_type=jnp.float32)
        ) * score_scale
        seen = (key_pos[None, :] <= query_pos[:, None])[None, :, :]
        score = jnp.where(seen, score, jnp.float32(-1e30))
        fresh = jnp.maximum(top, jnp.max(score, axis=2))
        weight = jnp.where(seen, jnp.exp(score - fresh[:, :, None]), jnp.float32(0.0))
        factor = jnp.exp(top - fresh)
        total = total * factor + jnp.sum(weight, axis=2)
        summed = summed * factor[:, :, None] + jnp.einsum(
            "htn,nl->htl",
            weight.astype(jnp.bfloat16),
            lat_piece,
            preferred_element_type=jnp.float32,
        )
        return (fresh, total, summed)

    start_carry = (
        jnp.full((local_heads, tok_rows), -1e30, jnp.float32),
        jnp.zeros((local_heads, tok_rows), jnp.float32),
        jnp.zeros((local_heads, tok_rows, latent.shape[1]), jnp.float32),
    )
    all_lat, all_rope = (
        lax.all_gather(latent, "seq", axis=0, tiled=True),
        lax.all_gather(key_rope, "seq", axis=0, tiled=True),
    )
    block = tok_rows * min(8, seq_count)
    steps_count = all_lat.shape[0] // block

    def visit(step, carry):
        begin = (step * block).astype(jnp.int32)
        lat_piece = lax.dynamic_slice_in_dim(all_lat, begin, block, 0)
        rope_piece = lax.dynamic_slice_in_dim(all_rope, begin, block, 0)
        return attend(carry, (lat_piece, rope_piece), begin)

    top, total, summed = lax.fori_loop(0, steps_count, visit, start_carry)
    context = (summed / total[:, :, None]).astype(jnp.bfloat16)
    per_head = jnp.einsum(
        "htl,hle->the", context, absorb_value, preferred_element_type=jnp.float32
    ).astype(jnp.bfloat16)
    heads_out = per_head.reshape(tok_rows, local_heads * per_head.shape[2])
    every_row = lax.all_gather(heads_out, "seq", axis=0, tiled=True)
    columns = jnp.dot(every_row, w_out, preferred_element_type=jnp.float32).astype(jnp.bfloat16)
    partial_value = lax.all_to_all(columns, "seq", split_axis=0, concat_axis=1, tiled=True).astype(
        jnp.float32
    )
    projected = lax.psum_scatter(
        partial_value.astype(jnp.bfloat16), "heads", scatter_dimension=0, tiled=True
    ).astype(jnp.float32)
    hidden = residual.astype(jnp.float32) + projected
    new_residual = hidden.astype(jnp.bfloat16)
    scale = lax.rsqrt(jnp.mean(hidden * hidden, axis=1, keepdims=True) + 1e-06)
    normed = (hidden * scale * norm_gain[None, :]).astype(jnp.bfloat16)
    return (new_residual, normed)


def solution(mesh):
    in_specs = (
        P("seq", "heads", None),
        P("seq", "heads", None),
        P("seq", None),
        P("seq", None),
        P("heads", None, None),
        P("heads", None, None),
        P("heads", "seq"),
        P(("seq", "heads"), None),
        P(),
        P(),
    )
    out_specs = (P(("seq", "heads"), None), P(("seq", "heads"), None))
    return jax.shard_map(
        per_device, mesh=mesh, in_specs=in_specs, out_specs=out_specs, check_vma=False
    )
```

profile of v0, /device:TPU:0, one launch (start us, length us, event | category | flops | bytes accessed | tf_op | source)
XLA Modules:
  0.0 225.6 jit_solution(14816708200302043049)
XLA Ops:
  7.2 0.7 all-gather.4.cloned.1.call-update
  8.0 24.1 %all-gather = bf16[16,72,64]{1,2,0:T(8,128)(2,1)S(1)} all-gather(bf16[1,72,64]{1,2,0:T(8,128)(2,1)} %bitcast.47), channel_id=1, replica_groups=mesh['heads'=2,'seq'=16] {'seq'}, dimensions={0}, use_global_device_ids=true | all-gather | bytes 156672 | tf_op jit(solution)/shard_map/all_gather | solution.py:73
  32.6 0.7 select_reduce_fusion.1
  33.4 4.7 %convolution_convert_fusion.1 = bf16[32,72,512]{2,1,0:T(8,128)(2,1)} fusion(bf16[32,128,512]{2,1,0:T(8,128)(2,1)} %param.16, bf16[72,32,128]{2,1,0:T(8,128)(2,1)} %param.12), kind=kOutput, calls=%fused_computation.41 | convolution fusion | flops 303169536 | bytes 7143424 | tf_op jit(solution)/shard_map/thd,hdl->htl/dot_general | solution.py:37
  38.0 13.4 %all-gather.4.cloned.1.call-done = bf16[1152,512]{1,0:T(8,128)(2,1)} async-done(((bf16[72,512]{1,0:T(8,128)(2,1)}), bf16[1152,512]{1,0:T(8,128)(2,1)}) %all-gather.4.cloned.1.call-update) | async-done | bytes 1179664 | tf_op jit(solution)/shard_map/all_gather | solution.py:72
  51.4 36.1 %while.20 = (s32[]{:T(128)}, f32[32,72]{1,0:T(8,128)S(1)}, f32[32,72]{1,0:T(8,128)S(1)}, f32[32,72,512]{2,1,0:T(8,128)}, s32[32]{0:T(128)S(1)}, /*index=5*/s32[7...) while((s32[]{:T(128)}, f32[32,72]{1,0:T(8,128)S(1)}, ...), condition=%wide.region_5.6_spmd.clone, body=%wide.region_1.5_spmd.clone.sunk | while | flops 2904706304 | bytes 68787400 | solution.py:84
  51.4 3.9 %fusion.59 = f32[576,32,72]{0,2,1:T(8,128)S(1)} fusion(bf16[32,72,512]{2,1,0:T(8,128)(2,1)} %get-tuple-element.413, bf16[1152,512]{1,0:T(8,128)(2,1)} %get-tuple-element.412, s32[]{:T(128)S(6)} %select_n.141), kind=kOutput, calls=%fused_computation.11.clone.1 | convolution fusion | flops 1358954496 | bytes 8257540 | tf_op jit(solution)/shard_map/while/body/eval_jaxpr/htl,nl->htn/dot_general | solution.py:47
  55.6 4.2 %fusion.61 = (f32[32,72]{1,0:T(8,128)S(1)}, f32[32,72,576]{2,1,0:T(8,128)}) fusion(f32[576,32,72]{0,2,1:T(8,128)S(1)} %fusion.59, bf16[32,72,64]{1,2,0:T(8,128)(2,1)S(1)} %copy-done.3, bf16[1152,64]{0,1:T(8,128)(2,1)S(1)} %get-tuple-element.414, s32[]{:T(128)S(6)} %select_n.141, pred[72,576]{1,0:T(8,128)(4,1)S(1)} %broadcast_compare_fusion.2), kind=kOutput, calls=%fused_computation.58.clone.1 | convolution fusion | flops 175175424 | bytes 11868164 | tf_op jit(solution)/shard_map/while/body/eval_jaxpr/htr,nr->htn/dot_general | solution.py:50
  59.9 4.1 %fusion.62 = f32[32,72]{1,0:T(8,128)S(1)} fusion(f32[32,72,576]{2,1,0:T(8,128)} %get-tuple-element.375, f32[32,72]{1,0:T(8,128)S(1)} %select_maximum_fusion.2, pred[72,576]{1,0:T(8,128)(4,1)S(1)} %broadcast_compare_fusion.2), kind=kLoop, calls=%fused_computation.3.clone.1 | loop fusion | flops 3979008 | bytes 5368320 | tf_op jit(solution)/shard_map/while/body/eval_jaxpr/reduce_sum | solution.py:57
  64.3 4.4 %fusion.64 = f32[32,72,512]{2,1,0:T(8,128)} fusion(f32[32,72,512]{2,1,0:T(8,128)} %get-tuple-element.395, f32[32,72]{1,0:T(8,128)S(1)} %get-tuple-element.377, pred[]{:T(512)S(6)} %compare.3, f32[32,72,576]{2,1,0:T(8,128)S(1)} %copy-done.1, f32[32,72]{1,0:T(8,128)S(1)} %select_maximum_fusion.2, pred[72,576]{1,0:T(8,128)(4,1)S(1)} %broadcast_compare_fusion.2, ...), kind=kOutput, calls=%fused_computation.5.clone.1 | convolution fusion | flops 1366474752 | bytes 16004101 | tf_op jit(solution)/shard_map/while/body/eval_jaxpr/htn,nl->htl/dot_general | solution.py:58
  68.6 3.9 %fusion.59 = f32[576,32,72]{0,2,1:T(8,128)S(1)} fusion(bf16[32,72,512]{2,1,0:T(8,128)(2,1)} %get-tuple-element.413, bf16[1152,512]{1,0:T(8,128)(2,1)} %get-tuple-element.412, s32[]{:T(128)S(6)} %select_n.141), kind=kOutput, calls=%fused_computation.11.clone.1 | convolution fusion | flops 1358954496 | bytes 8257540 | tf_op jit(solution)/shard_map/while/body/eval_jaxpr/htl,nl->htn/dot_general | solution.py:47
  72.8 4.2 %fusion.61 = (f32[32,72]{1,0:T(8,128)S(1)}, f32[32,72,576]{2,1,0:T(8,128)}) fusion(f32[576,32,72]{0,2,1:T(8,128)S(1)} %fusion.59, bf16[32,72,64]{1,2,0:T(8,128)(2,1)S(1)} %copy-done.3, bf16[1152,64]{0,1:T(8,128)(2,1)S(1)} %get-tuple-element.414, s32[]{:T(128)S(6)} %select_n.141, pred[72,576]{1,0:T(8,128)(4,1)S(1)} %broadcast_compare_fusion.2), kind=kOutput, calls=%fused_computation.58.clone.1 | convolution fusion | flops 175175424 | bytes 11868164 | tf_op jit(solution)/shard_map/while/body/eval_jaxpr/htr,nr->htn/dot_general | solution.py:50
  77.1 4.1 %fusion.62 = f32[32,72]{1,0:T(8,128)S(1)} fusion(f32[32,72,576]{2,1,0:T(8,128)} %get-tuple-element.375, f32[32,72]{1,0:T(8,128)S(1)} %select_maximum_fusion.2, pred[72,576]{1,0:T(8,128)(4,1)S(1)} %broadcast_compare_fusion.2), kind=kLoop, calls=%fused_computation.3.clone.1 | loop fusion | flops 3979008 | bytes 5368320 | tf_op jit(solution)/shard_map/while/body/eval_jaxpr/reduce_sum | solution.py:57
  81.5 6.0 %fusion.64 = f32[32,72,512]{2,1,0:T(8,128)} fusion(f32[32,72,512]{2,1,0:T(8,128)} %get-tuple-element.395, f32[32,72]{1,0:T(8,128)S(1)} %get-tuple-element.377, pred[]{:T(512)S(6)} %compare.3, f32[32,72,576]{2,1,0:T(8,128)S(1)} %copy-done.1, f32[32,72]{1,0:T(8,128)S(1)} %select_maximum_fusion.2, pred[72,576]{1,0:T(8,128)(4,1)S(1)} %broadcast_compare_fusion.2, ...), kind=kOutput, calls=%fused_computation.5.clone.1 | convolution fusion | flops 1366474752 | bytes 16004101 | tf_op jit(solution)/shard_map/while/body/eval_jaxpr/htn,nl->htl/dot_general | solution.py:58
  87.5 4.6 %fusion.31 = bf16[32,9,8,128]{3,2,1,0:T(8,128)(2,1)S(1)} fusion(bf16[32,512,128]{2,1,0:T(8,128)(2,1)} %param.17, f32[32,72,512]{2,1,0:T(8,128)} %get-tuple-element.248, f32[32,72]{1,0:T(8,128)S(1)} %get-tuple-element.249), kind=kOutput, calls=%fused_computation.43 | convolution fusion | flops 304644096 | bytes 9511936 | tf_op jit(solution)/shard_map/htl,hle->the/dot_general | solution.py:86
  92.1 0.9 copy.42
  93.1 79.9 %all-gather.6.cloned.1.call-done = bf16[1152,4096]{1,0:T(8,128)(2,1)} async-done(((bf16[72,4096]{1,0:T(8,128)(2,1)}), bf16[1152,4096]{1,0:T(8,128)(2,1)}) %all-gather.6.cloned.1.call-update) | async-done | bytes 9437200 | tf_op jit(solution)/shard_map/all_gather | solution.py:90
  173.0 6.7 %convolution_convert_fusion = bf16[1152,224]{0,1:T(8,128)(2,1)S(1)} fusion(bf16[1152,4096]{1,0:T(8,128)(2,1)} %all-gather.6.cloned.1.call-done, bf16[4096,224]{0,1:T(8,128)(2,1)S(1)} %copy-done), kind=kOutput, calls=%fused_computation.39 | convolution fusion | flops 2114187264 | bytes 11788288 | tf_op jit(solution)/shard_map/dot_general | solution.py:91
  180.0 20.2 %all_to_all.19 = bf16[16,72,224]{2,1,0:T(8,128)(2,1)S(1)} all-to-all(bf16[16,72,224]{2,1,0:T(8,128)(2,1)S(1)} %bitcast.45), channel_id=1, replica_groups=mesh['heads'=2,'seq'=16] {'seq'}, dimensions={0} | all-to-all | bytes 1032192 | tf_op jit(solution)/shard_map/all_to_all | solution.py:92
  200.3 1.0 all_to_all.17
  201.3 11.8 %fusion = bf16[40,3584]{1,0:T(8,128)(2,1)S(1)} fusion(bf16[72,3584]{1,0:T(8,128)(2,1)S(1)} %all_to_all.17), kind=kCustom, calls=%all-reduce-scatter | all-reduce-scatter fusion | flops 286721 | bytes 803328
  213.1 2.5 %collective-permute-start = (bf16[4,3584]{1,0:T(4,128)(2,1)S(1)}, bf16[4,3584]{1,0:T(4,128)(2,1)S(1)}, u32[]{:S(2)}, u32[]{:S(2)}) collective-permute-start(bf16[4,3584]{1,0:T(4,128)(2,1)S(1)} %slice), channel_id=1, source_target_pairs={{0,16},{1,17},{2,18},{3,19},{4,20},{5,21},{6,22},{7,23},{8,24},{9,... | collective-permute-start | bytes 86024
  215.6 0.6 dynamic-slice.4
  217.8 1.0 multiply_convert_fusion
  (53 shorter events, 3.0 us)
Async XLA Ops:
  7.2 165.8 %copy-start = (bf16[4096,224]{0,1:T(8,128)(2,1)S(1)}, bf16[4096,224]{0,1:T(8,128)(2,1)}, u32[]{:S(2)}) copy-start(bf16[4096,224]{0,1:T(8,128)(2,1)} %param.18) | copy-start | bytes 5505028
  7.2 44.2 %copy-start.6 = (s32[32]{0:T(128)S(1)}, s32[32]{0:T(128)}, u32[]{:S(2)}) copy-start(s32[32]{0:T(128)} %param.21) | copy-start | bytes 388
  7.2 44.2 %all-gather.4.cloned.1.call-start = ((), (), s32[]{:S(2)}) async-start(), calls=%async_computation.1 | async-start | bytes 1253376 | tf_op jit(solution)/shard_map/all_gather | solution.py:72
  7.9 165.1 %all-gather.6.cloned.1.call-start = ((), (), s32[]{:S(2)}) async-start(), calls=%async_computation.2 | async-start | bytes 10027008 | tf_op jit(solution)/shard_map/all_gather | solution.py:90
  51.4 4.2 %copy-start.3 = (bf16[32,72,64]{1,2,0:T(8,128)(2,1)S(1)}, bf16[32,72,64]{1,2,0:T(8,128)(2,1)}, u32[]{:S(2)}) copy-start(bf16[32,72,64]{1,2,0:T(8,128)(2,1)} %get-tuple-element.415) | copy-start | bytes 884740 | tf_op jit(solution)/shard_map/while
  55.6 8.4 %copy-start.2 = (bf16[1152,512]{1,0:T(8,128)(2,1)S(1)}, bf16[1152,512]{1,0:T(8,128)(2,1)}, u32[]{:S(2)}) copy-start(bf16[1152,512]{1,0:T(8,128)(2,1)} %get-tuple-element.412) | copy-start | bytes 3538948 | tf_op jit(solution)/shard_map/while
  59.8 4.4 %copy-start.1 = (f32[32,72,576]{2,1,0:T(8,128)S(1)}, f32[32,72,576]{2,1,0:T(8,128)}, u32[]{:S(2)}) copy-start(f32[32,72,576]{2,1,0:T(8,128)} %get-tuple-element.375) | copy-start | bytes 15925252 | tf_op jit(solution)/shard_map/while
  68.6 4.2 %copy-start.3 = (bf16[32,72,64]{1,2,0:T(8,128)(2,1)S(1)}, bf16[32,72,64]{1,2,0:T(8,128)(2,1)}, u32[]{:S(2)}) copy-start(bf16[32,72,64]{1,2,0:T(8,128)(2,1)} %get-tuple-element.415) | copy-start | bytes 884740 | tf_op jit(solution)/shard_map/while
  72.8 8.4 %copy-start.2 = (bf16[1152,512]{1,0:T(8,128)(2,1)S(1)}, bf16[1152,512]{1,0:T(8,128)(2,1)}, u32[]{:S(2)}) copy-start(bf16[1152,512]{1,0:T(8,128)(2,1)} %get-tuple-element.412) | copy-start | bytes 3538948 | tf_op jit(solution)/shard_map/while
  77.1 4.4 %copy-start.1 = (f32[32,72,576]{2,1,0:T(8,128)S(1)}, f32[32,72,576]{2,1,0:T(8,128)}, u32[]{:S(2)}) copy-start(f32[32,72,576]{2,1,0:T(8,128)} %get-tuple-element.375) | copy-start | bytes 15925252 | tf_op jit(solution)/shard_map/while
  179.8 35.8 %copy-start.7 = (u32[32]{0:T(128)S(1)}, u32[32]{0:T(128)}, u32[]{:S(2)}) copy-start(u32[32]{0:T(128)} %constant.152) | copy-start | bytes 388
  179.8 37.8 %copy-start.4 = (bf16[36,3584]{1,0:T(8,128)(2,1)S(1)}, bf16[36,3584]{1,0:T(8,128)(2,1)}, u32[]{:S(2)}) copy-start(bf16[36,3584]{1,0:T(8,128)(2,1)} %param.19) | copy-start | bytes 774148
  179.8 38.0 %copy-start.5 = (f32[3584]{0:T(1024)S(1)}, f32[3584]{0:T(1024)}, u32[]{:S(2)}) copy-start(f32[3584]{0:T(1024)} %param.20) | copy-start | bytes 43012
  213.1 4.0 %collective-permute-start = (bf16[4,3584]{1,0:T(4,128)(2,1)S(1)}, bf16[4,3584]{1,0:T(4,128)(2,1)S(1)}, u32[]{:S(2)}, u32[]{:S(2)}) collective-permute-start(bf16[4,3584]{1,0:T(4,128)(2,1)S(1)} %slice), channel_id=1, source_target_pairs={{0,16},{1,17},{2,18},{3,19},{4,20},{5,21},{6,22},{7,23},{8,24},{9,... | collective-permute-start | bytes 86024
Sparse Core Ops, SparseCore 0:
  10.3 41.0 all-gather.3
  93.2 79.7 all-gather.5
where the time goes:
time: 226 us
  waiting for transfers between devices  94.3 us (42%)
  blocking collectives  56.1 us (25%)
  matrix products  42.8 us (19%)
  between operations  14.9 us (7%)
  other arithmetic  10.7 us (5%)
  local copies, waits for them, and re-layouts  4.29 us (2%)
  starting transfers between devices  2.54 us (1%)
    all_gather x1, waiting for transfers between devices, per_device(): every_row = lax.all_gather(heads_out, 'seq', axis=0, tiled=True)  79.9 us
    all_gather x1, blocking collectives, per_device(): lax.all_gather(key_rope, 'seq', axis=0, tiled=True)  24.1 us
    all_to_all x1, blocking collectives, per_device(): lax.all_to_all(columns, 'seq', split_axis=0, concat_axis=1, tiled=True)  20.2 us
    all_gather x1, waiting for transfers between devices, per_device(): lax.all_gather(latent, 'seq', axis=0, tiled=True)  13.4 us
    unnamed x1, blocking collectives  11.8 us
    dot_general x2, matrix products, attend(): jnp.einsum('htn,nl->htl', weight.astype(jnp.bfloat16), lat_piece, preferr...  10.4 us
    dot_general x2, matrix products, attend(): jnp.einsum('htr,nr->htn', rotary, rope_piece, preferred_element_type=jnp....  8.46 us
    reduce_sum x2, other arithmetic, attend(): total = total * factor + jnp.sum(weight, axis=2)  8.21 us
  transfers between devices with their start and end apart: 3, of which 3 were waited for; matrix products, arithmetic and copies ran while one was open for 3% of the time, Pallas kernels for 0%

commit v1 on v0

--- a/solution.py
+++ b/solution.py
@@ -89,9 +89,11 @@
     heads_out = per_head.reshape(tok_rows, local_heads * per_head.shape[2])
     every_row = lax.all_gather(heads_out, "seq", axis=0, tiled=True)
     columns = jnp.dot(every_row, w_out, preferred_element_type=jnp.float32).astype(jnp.bfloat16)
-    partial_value = lax.all_to_all(columns, "seq", split_axis=0, concat_axis=1, tiled=True).astype(
-        jnp.float32
+    keep_up_goods = lambda vec: jnp.concatenate(
+        lax.all_to_all(jnp.stack(jnp.split(vec, lax.axis_size("seq"), 0), axis=0), "seq", 0, 0),
+        axis=1,
     )
+    partial_value = keep_up_goods(columns).astype(jnp.float32)
     projected = lax.psum_scatter(
         partial_value.astype(jnp.bfloat16), "heads", scatter_dimension=0, tiled=True
     ).astype(jnp.float32)

time: 226 us -> 238 us (1.053)
  local copies, waits for them, and re-layouts: 4.29 us -> 16.7 us
    unnamed x14 -> x29, local copies, waits for them, and re-layouts: 1.33 us -> 11.8 us
where the time goes in v1:
time: 238 us
  waiting for transfers between devices  94.3 us (40%)
  blocking collectives  56.1 us (24%)
  matrix products  42.8 us (18%)
  local copies, waits for them, and re-layouts  16.7 us (7%)
  between operations  14.9 us (6%)
  other arithmetic  10.7 us (4%)
  starting transfers between devices  2.54 us (1%)
    all_gather x1, waiting for transfers between devices, per_device(): every_row = lax.all_gather(heads_out, 'seq', axis=0, tiled=True)  79.9 us
    all_gather x1, blocking collectives, per_device(): lax.all_gather(key_rope, 'seq', axis=0, tiled=True)  24.1 us
    all_to_all x1, blocking collectives, per_device(): lax.all_to_all(jnp.stack(jnp.split(vec, lax.axis_size('seq'), 0), axis=0)...  20.2 us
    all_gather x1, waiting for transfers between devices, per_device(): lax.all_gather(latent, 'seq', axis=0, tiled=True)  13.4 us
    unnamed x29, local copies, waits for them, and re-layouts  11.8 us
    unnamed x1, blocking collectives  11.8 us
    dot_general x2, matrix products, attend(): jnp.einsum('htn,nl->htl', weight.astype(jnp.bfloat16), lat_piece, preferr...  10.4 us
    dot_general x2, matrix products, attend(): jnp.einsum('htr,nr->htn', rotary, rope_piece, preferred_element_type=jnp....  8.46 us
  transfers between devices with their start and end apart: 3, of which 3 were waited for; matrix products, arithmetic and copies ran while one was open for 3% of the time, Pallas kernels for 0%

profile of v1, /device:TPU:0, one launch (start us, length us, event | category | flops | bytes accessed | tf_op | source)
XLA Modules:
  0.0 238.1 jit_solution(13284421098275285304)
XLA Ops:
  8.0 24.1 %all-gather = bf16[16,72,64]{1,2,0:T(8,128)(2,1)S(1)} all-gather(bf16[1,72,64]{1,2,0:T(8,128)(2,1)} %bitcast.109), channel_id=1, replica_groups=mesh['heads'=2,'seq'=16] {'seq'}, dimensions={0}, use_global_device_ids=true | all-gather | bytes 156672 | tf_op jit(solution)/shard_map/all_gather | solution.py:73
  32.6 0.7 select_reduce_fusion.1
  33.4 4.7 %convolution_convert_fusion.1 = bf16[32,72,512]{2,1,0:T(8,128)(2,1)} fusion(bf16[32,128,512]{2,1,0:T(8,128)(2,1)} %param.16, bf16[72,32,128]{2,1,0:T(8,128)(2,1)} %param.12), kind=kOutput, calls=%fused_computation.41 | convolution fusion | flops 303169536 | bytes 7143424 | tf_op jit(solution)/shard_map/thd,hdl->htl/dot_general | solution.py:37
  38.0 13.4 %all-gather.4.cloned.1.call-done = bf16[1152,512]{1,0:T(8,128)(2,1)} async-done(((bf16[72,512]{1,0:T(8,128)(2,1)}), bf16[1152,512]{1,0:T(8,128)(2,1)}) %all-gather.4.cloned.1.call-update) | async-done | bytes 1179664 | tf_op jit(solution)/shard_map/all_gather | solution.py:72
  51.4 36.1 %while.20 = (s32[]{:T(128)}, f32[32,72]{1,0:T(8,128)S(1)}, f32[32,72]{1,0:T(8,128)S(1)}, f32[32,72,512]{2,1,0:T(8,128)}, s32[32]{0:T(128)S(1)}, /*index=5*/s32[7...) while((s32[]{:T(128)}, f32[32,72]{1,0:T(8,128)S(1)}, ...), condition=%wide.region_5.6_spmd.clone, body=%wide.region_1.5_spmd.clone.sunk | while | flops 2904706304 | bytes 68787400 | solution.py:84
  51.4 3.9 %fusion.75 = f32[576,32,72]{0,2,1:T(8,128)S(1)} fusion(bf16[32,72,512]{2,1,0:T(8,128)(2,1)} %get-tuple-element.413, bf16[1152,512]{1,0:T(8,128)(2,1)} %get-tuple-element.412, s32[]{:T(128)S(6)} %select_n.141), kind=kOutput, calls=%fused_computation.11.clone.1 | convolution fusion | flops 1358954496 | bytes 8257540 | tf_op jit(solution)/shard_map/while/body/eval_jaxpr/htl,nl->htn/dot_general | solution.py:47
  55.6 4.2 %fusion.77 = (f32[32,72]{1,0:T(8,128)S(1)}, f32[32,72,576]{2,1,0:T(8,128)}) fusion(f32[576,32,72]{0,2,1:T(8,128)S(1)} %fusion.75, bf16[32,72,64]{1,2,0:T(8,128)(2,1)S(1)} %copy-done.3, bf16[1152,64]{0,1:T(8,128)(2,1)S(1)} %get-tuple-element.414, s32[]{:T(128)S(6)} %select_n.141, pred[72,576]{1,0:T(8,128)(4,1)S(1)} %broadcast_compare_fusion.2), kind=kOutput, calls=%fused_computation.90.clone.1 | convolution fusion | flops 175175424 | bytes 11868164 | tf_op jit(solution)/shard_map/while/body/eval_jaxpr/htr,nr->htn/dot_general | solution.py:50
  59.9 4.1 %fusion.78 = f32[32,72]{1,0:T(8,128)S(1)} fusion(f32[32,72,576]{2,1,0:T(8,128)} %get-tuple-element.375, f32[32,72]{1,0:T(8,128)S(1)} %select_maximum_fusion.2, pred[72,576]{1,0:T(8,128)(4,1)S(1)} %broadcast_compare_fusion.2), kind=kLoop, calls=%fused_computation.3.clone.1 | loop fusion | flops 3979008 | bytes 5368320 | tf_op jit(solution)/shard_map/while/body/eval_jaxpr/reduce_sum | solution.py:57
  64.3 4.4 %fusion.80 = f32[32,72,512]{2,1,0:T(8,128)} fusion(f32[32,72,512]{2,1,0:T(8,128)} %get-tuple-element.395, f32[32,72]{1,0:T(8,128)S(1)} %get-tuple-element.377, pred[]{:T(512)S(6)} %compare.3, f32[32,72,576]{2,1,0:T(8,128)S(1)} %copy-done.1, f32[32,72]{1,0:T(8,128)S(1)} %select_maximum_fusion.2, pred[72,576]{1,0:T(8,128)(4,1)S(1)} %broadcast_compare_fusion.2, ...), kind=kOutput, calls=%fused_computation.5.clone.1 | convolution fusion | flops 1366474752 | bytes 16004101 | tf_op jit(solution)/shard_map/while/body/eval_jaxpr/htn,nl->htl/dot_general | solution.py:58
  68.6 3.9 %fusion.75 = f32[576,32,72]{0,2,1:T(8,128)S(1)} fusion(bf16[32,72,512]{2,1,0:T(8,128)(2,1)} %get-tuple-element.413, bf16[1152,512]{1,0:T(8,128)(2,1)} %get-tuple-element.412, s32[]{:T(128)S(6)} %select_n.141), kind=kOutput, calls=%fused_computation.11.clone.1 | convolution fusion | flops 1358954496 | bytes 8257540 | tf_op jit(solution)/shard_map/while/body/eval_jaxpr/htl,nl->htn/dot_general | solution.py:47
  72.8 4.2 %fusion.77 = (f32[32,72]{1,0:T(8,128)S(1)}, f32[32,72,576]{2,1,0:T(8,128)}) fusion(f32[576,32,72]{0,2,1:T(8,128)S(1)} %fusion.75, bf16[32,72,64]{1,2,0:T(8,128)(2,1)S(1)} %copy-done.3, bf16[1152,64]{0,1:T(8,128)(2,1)S(1)} %get-tuple-element.414, s32[]{:T(128)S(6)} %select_n.141, pred[72,576]{1,0:T(8,128)(4,1)S(1)} %broadcast_compare_fusion.2), kind=kOutput, calls=%fused_computation.90.clone.1 | convolution fusion | flops 175175424 | bytes 11868164 | tf_op jit(solution)/shard_map/while/body/eval_jaxpr/htr,nr->htn/dot_general | solution.py:50
  77.1 4.1 %fusion.78 = f32[32,72]{1,0:T(8,128)S(1)} fusion(f32[32,72,576]{2,1,0:T(8,128)} %get-tuple-element.375, f32[32,72]{1,0:T(8,128)S(1)} %select_maximum_fusion.2, pred[72,576]{1,0:T(8,128)(4,1)S(1)} %broadcast_compare_fusion.2), kind=kLoop, calls=%fused_computation.3.clone.1 | loop fusion | flops 3979008 | bytes 5368320 | tf_op jit(solution)/shard_map/while/body/eval_jaxpr/reduce_sum | solution.py:57
  81.5 6.0 %fusion.80 = f32[32,72,512]{2,1,0:T(8,128)} fusion(f32[32,72,512]{2,1,0:T(8,128)} %get-tuple-element.395, f32[32,72]{1,0:T(8,128)S(1)} %get-tuple-element.377, pred[]{:T(512)S(6)} %compare.3, f32[32,72,576]{2,1,0:T(8,128)S(1)} %copy-done.1, f32[32,72]{1,0:T(8,128)S(1)} %select_maximum_fusion.2, pred[72,576]{1,0:T(8,128)(4,1)S(1)} %broadcast_compare_fusion.2, ...), kind=kOutput, calls=%fused_computation.5.clone.1 | convolution fusion | flops 1366474752 | bytes 16004101 | tf_op jit(solution)/shard_map/while/body/eval_jaxpr/htn,nl->htl/dot_general | solution.py:58
  87.5 4.6 %fusion.31 = bf16[32,9,8,128]{3,2,1,0:T(8,128)(2,1)S(1)} fusion(bf16[32,512,128]{2,1,0:T(8,128)(2,1)} %param.17, f32[32,72,512]{2,1,0:T(8,128)} %get-tuple-element.248, f32[32,72]{1,0:T(8,128)S(1)} %get-tuple-element.249), kind=kOutput, calls=%fused_computation.43 | convolution fusion | flops 304644096 | bytes 9511936 | tf_op jit(solution)/shard_map/htl,hle->the/dot_general | solution.py:86
  92.1 0.9 copy.36
  93.1 79.9 %all-gather.6.cloned.1.call-done = bf16[1152,4096]{1,0:T(8,128)(2,1)} async-done(((bf16[72,4096]{1,0:T(8,128)(2,1)}), bf16[1152,4096]{1,0:T(8,128)(2,1)}) %all-gather.6.cloned.1.call-update) | async-done | bytes 9437200 | tf_op jit(solution)/shard_map/all_gather | solution.py:90
  173.0 6.7 %convolution_convert_fusion = bf16[1152,224]{0,1:T(8,128)(2,1)S(1)} fusion(bf16[1152,4096]{1,0:T(8,128)(2,1)} %all-gather.6.cloned.1.call-done, bf16[4096,224]{0,1:T(8,128)(2,1)S(1)} %copy-done), kind=kOutput, calls=%fused_computation.39 | convolution fusion | flops 2114187264 | bytes 11788288 | tf_op jit(solution)/shard_map/dot_general | solution.py:91
  186.0 0.7 fusion.40
  191.0 1.5 copy.30
  192.5 20.2 %all_to_all.5 = bf16[16,72,224]{2,1,0:T(8,128)(2,1)S(1)} all-to-all(bf16[16,72,224]{2,1,0:T(8,128)(2,1)S(1)} %copy.30), channel_id=1, replica_groups=mesh['heads'=2,'seq'=16] {'seq'}, dimensions={0} | all-to-all | bytes 1032192 | tf_op jit(solution)/shard_map/all_to_all | solution.py:93
  212.8 1.0 reshape.99
  213.7 11.8 %fusion = bf16[40,3584]{1,0:T(8,128)(2,1)S(1)} fusion(bf16[72,3584]{1,0:T(8,128)(2,1)S(1)} %reshape.99), kind=kCustom, calls=%all-reduce-scatter | all-reduce-scatter fusion | flops 286721 | bytes 803328
  225.6 2.5 %collective-permute-start = (bf16[4,3584]{1,0:T(4,128)(2,1)S(1)}, bf16[4,3584]{1,0:T(4,128)(2,1)S(1)}, u32[]{:S(2)}, u32[]{:S(2)}) collective-permute-start(bf16[4,3584]{1,0:T(4,128)(2,1)S(1)} %slice), channel_id=1, source_target_pairs={{0,16},{1,17},{2,18},{3,19},{4,20},{5,21},{6,22},{7,23},{8,24},{9,... | collective-permute-start | bytes 86024
  230.3 1.0 multiply_convert_fusion
  (69 shorter events, 14.5 us)
Async XLA Ops:
  7.2 165.8 %copy-start = (bf16[4096,224]{0,1:T(8,128)(2,1)S(1)}, bf16[4096,224]{0,1:T(8,128)(2,1)}, u32[]{:S(2)}) copy-start(bf16[4096,224]{0,1:T(8,128)(2,1)} %param.18) | copy-start | bytes 5505028
  7.2 44.2 %copy-start.6 = (s32[32]{0:T(128)S(1)}, s32[32]{0:T(128)}, u32[]{:S(2)}) copy-start(s32[32]{0:T(128)} %param.21) | copy-start | bytes 388
  7.2 44.2 %all-gather.4.cloned.1.call-start = ((), (), s32[]{:S(2)}) async-start(), calls=%async_computation.1 | async-start | bytes 1253376 | tf_op jit(solution)/shard_map/all_gather | solution.py:72
  7.9 165.1 %all-gather.6.cloned.1.call-start = ((), (), s32[]{:S(2)}) async-start(), calls=%async_computation.2 | async-start | bytes 10027008 | tf_op jit(solution)/shard_map/all_gather | solution.py:90
  51.4 4.2 %copy-start.3 = (bf16[32,72,64]{1,2,0:T(8,128)(2,1)S(1)}, bf16[32,72,64]{1,2,0:T(8,128)(2,1)}, u32[]{:S(2)}) copy-start(bf16[32,72,64]{1,2,0:T(8,128)(2,1)} %get-tuple-element.415) | copy-start | bytes 884740 | tf_op jit(solution)/shard_map/while
  55.6 8.4 %copy-start.2 = (bf16[1152,512]{1,0:T(8,128)(2,1)S(1)}, bf16[1152,512]{1,0:T(8,128)(2,1)}, u32[]{:S(2)}) copy-start(bf16[1152,512]{1,0:T(8,128)(2,1)} %get-tuple-element.412) | copy-start | bytes 3538948 | tf_op jit(solution)/shard_map/while
  59.8 4.4 %copy-start.1 = (f32[32,72,576]{2,1,0:T(8,128)S(1)}, f32[32,72,576]{2,1,0:T(8,128)}, u32[]{:S(2)}) copy-start(f32[32,72,576]{2,1,0:T(8,128)} %get-tuple-element.375) | copy-start | bytes 15925252 | tf_op jit(solution)/shard_map/while
  68.6 4.2 %copy-start.3 = (bf16[32,72,64]{1,2,0:T(8,128)(2,1)S(1)}, bf16[32,72,64]{1,2,0:T(8,128)(2,1)}, u32[]{:S(2)}) copy-start(bf16[32,72,64]{1,2,0:T(8,128)(2,1)} %get-tuple-element.415) | copy-start | bytes 884740 | tf_op jit(solution)/shard_map/while
  72.8 8.4 %copy-start.2 = (bf16[1152,512]{1,0:T(8,128)(2,1)S(1)}, bf16[1152,512]{1,0:T(8,128)(2,1)}, u32[]{:S(2)}) copy-start(bf16[1152,512]{1,0:T(8,128)(2,1)} %get-tuple-element.412) | copy-start | bytes 3538948 | tf_op jit(solution)/shard_map/while
  77.1 4.4 %copy-start.1 = (f32[32,72,576]{2,1,0:T(8,128)S(1)}, f32[32,72,576]{2,1,0:T(8,128)}, u32[]{:S(2)}) copy-start(f32[32,72,576]{2,1,0:T(8,128)} %get-tuple-element.375) | copy-start | bytes 15925252 | tf_op jit(solution)/shard_map/while
  179.8 48.3 %copy-start.7 = (u32[32]{0:T(128)S(1)}, u32[32]{0:T(128)}, u32[]{:S(2)}) copy-start(u32[32]{0:T(128)} %constant.152) | copy-start | bytes 388
  179.8 50.2 %copy-start.4 = (bf16[36,3584]{1,0:T(8,128)(2,1)S(1)}, bf16[36,3584]{1,0:T(8,128)(2,1)}, u32[]{:S(2)}) copy-start(bf16[36,3584]{1,0:T(8,128)(2,1)} %param.19) | copy-start | bytes 774148
  179.8 50.5 %copy-start.5 = (f32[3584]{0:T(1024)S(1)}, f32[3584]{0:T(1024)}, u32[]{:S(2)}) copy-start(f32[3584]{0:T(1024)} %param.20) | copy-start | bytes 43012
  225.6 4.0 %collective-permute-start = (bf16[4,3584]{1,0:T(4,128)(2,1)S(1)}, bf16[4,3584]{1,0:T(4,128)(2,1)S(1)}, u32[]{:S(2)}, u32[]{:S(2)}) collective-permute-start(bf16[4,3584]{1,0:T(4,128)(2,1)S(1)} %slice), channel_id=1, source_target_pairs={{0,16},{1,17},{2,18},{3,19},{4,20},{5,21},{6,22},{7,23},{8,24},{9,... | collective-permute-start | bytes 86024
Sparse Core Ops, SparseCore 0:
  10.3 41.0 all-gather.3
  93.2 79.7 all-gather.5
